TPU v7x, 128 devices: a whole 4x4x4 slice. The times are simulated.
128 devices in a mesh: high: 8 (over x, core), low: 16 (over z, y).
Axes of the slice: x: 4, y: 4, z: 4, core: 2. Of those that a mesh axis runs over, the one named last changes fastest.
Arguments:
- wave_parts: float32 [2, 2048, 128, 128], P(None, ('high', 'low')), may hold values from -6 to 6
- level_table: float32 [2048, 128, 128], P(('high', 'low')), may hold values from -2 to 2
- diagonal_angles: float32 [2, 128], replicated, may hold values from 0.3 to 1.2
- turn_angles: float32 [2, 4], replicated, may hold values from 0.3 to 1.2
Outputs:
- state_after: float32 [2, 2048, 128, 128], P(None, ('high', 'low'))
All inputs are finite; a program needn't handle non-finite values.
Results may differ from a plain program's by a relative error of at most 0.0003.
Values sent between devices are 32-bit elements.
No kernel may reach another device: no remote copies, remote signals or barrier semaphores. Data moves between devices by JAX's collectives and lax.ppermute only.
A program may use at most 64 MiB of HBM per device.

v0:
```python
import jax
import jax.numpy as jnp
from jax import lax
from jax.experimental import pallas as pl
from jax.experimental.pallas import tpu as pltpu
from jax.sharding import PartitionSpec as P

HIGH_LOW = ("high", "low")
DEVICES = 128
BLOCKS = 16
ROWS = 128
LANES = 128
CHUNK = 16
F32 = jnp.float32
BF16 = jnp.bfloat16

COS = (0.9999999403953552, -0.4999995529651642, 0.04166578873991966,
       -0.0013882378116250038, 2.4582879632362165e-05, -2.4136278398145805e-07)
SIN = (1.0, -0.16666662693023682, 0.008333264850080013,
       -0.0001983620022656396, 2.7387263799028005e-06, -2.2399454735477775e-08)


def poly(coefficients, z):
    total = coefficients[-1] * z + coefficients[-2]
    for c in coefficients[-3::-1]:
        total = total * z + c
    return total


def cos_sin(x):
    z = x * x
    return poly(COS, z), x * poly(SIN, z)


def angle_parts(turn_ref, layer):
    return [cos_sin(jnp.full((1, LANES), turn_ref[layer, g], F32)) for g in range(4)]


def power(x, n):
    total = x
    for _ in range(n - 1):
        total = total * x
    return total


def rotation(parts, scale, transposed):
    row = lax.broadcasted_iota(jnp.int32, (128, 128), 0)
    col = lax.broadcasted_iota(jnp.int32, (128, 128), 1)
    out, come = (col, row) if transposed else (row, col)
    total = jnp.broadcast_to(scale, (128, 128))
    for k, (c, s) in enumerate(parts):
        place = 1 << (6 - k)
        same = ((out ^ come) & place) == 0
        signed = jnp.where((out & place) != 0, -s, s)
        total = total * jnp.where(same, c, signed)
    return total


def split(x):
    top = x.astype(BF16)
    return top, (x - top.astype(F32)).astype(BF16)


def left_matrix(parts, scale):
    top, rest = split(rotation(parts, scale, False))
    zero = jnp.zeros_like(top)
    return jnp.concatenate(
        [jnp.concatenate([top, top], 1), jnp.concatenate([rest, zero], 1)], 0
    )


def right_matrix(parts, scale):
    top, rest = split(rotation(parts, scale, True))
    zero = jnp.zeros_like(top)
    return jnp.concatenate(
        [jnp.concatenate([top, rest], 1), jnp.concatenate([top, zero], 1)], 0
    )


def mix_rows_lanes(re, im, left, right):
    re_top, re_rest = split(re)
    im_top, im_rest = split(im)
    block = jnp.concatenate(
        [jnp.concatenate([re_top, im_top], 1), jnp.concatenate([re_rest, im_rest], 1)], 0
    )
    both = jnp.dot(left, block, preferred_element_type=F32)
    both = both[:128] + both[128:]
    re_top, re_rest = split(both[:, :128])
    im_top, im_rest = split(both[:, 128:])
    block = jnp.concatenate(
        [jnp.concatenate([re_top, re_rest], 1), jnp.concatenate([im_top, im_rest], 1)], 0
    )
    both = jnp.dot(block, right, preferred_element_type=F32)
    both = both[:, :128] + both[:, 128:]
    return both[:128], both[128:]


def butterflies(values, tangents):
    values = list(values)
    for k, t in enumerate(tangents):
        apart = len(values) >> (k + 1)
        for i in range(len(values)):
            if not i & apart:
                u, v = values[i], values[i + apart]
                values[i], values[i + apart] = u + t * v, v - t * u
    return values


def count_bits(x, bits):
    total = x & 1
    for k in range(1, bits):
        total = total + ((x >> k) & 1)
    return total


def device_bits():
    return count_bits(lax.axis_index("high"), 3) + count_bits(lax.axis_index("low"), 4)


def set_phases(odd_ref, re_sign_ref, im_sign_ref, rows, low_rows, back):
    row = lax.broadcasted_iota(jnp.int32, (rows, LANES), 0)
    lane = lax.broadcasted_iota(jnp.int32, (rows, LANES), 1)
    bits = count_bits(row, low_rows) + count_bits(lane, 7)
    for k in range(4):
        p = (bits + k) & 3
        odd_ref[k] = (p & 1).astype(F32)
        plus, minus = (1 - (p & 2)).astype(F32), (1 - ((p + 1) & 2)).astype(F32)
        re_sign_ref[k] = minus if back else plus
        im_sign_ref[k] = plus if back else minus


def first_kernel(turn_ref, angle_ref, wave_ref, level_ref, out_ref, wave, left, right,
                 odd, re_sign, im_sign, wave_sem, level_sem):
    steps = 8
    per = BLOCKS // steps

    def wave_copy(i):
        return pltpu.make_async_copy(
            wave_ref.at[:, pl.ds(i * per, per)], wave.at[i], wave_sem.at[i]
        )

    def level_copy(i):
        return pltpu.make_async_copy(
            level_ref.at[pl.ds(i * per * 8, per * 8)],
            out_ref.at[pl.ds(i * per * 8, per * 8), pl.ds(2 * CHUNK, CHUNK)],
            level_sem.at[i],
        )

    for i in range(steps):
        level_copy(i).start()
        wave_copy(i).start()

    parts = angle_parts(turn_ref, 0)
    (c0, s0), (c1, s1), (c2, s2), (c3, s3) = parts
    left[...] = left_matrix([parts[1]] * 7, jnp.ones_like(c1))
    right[...] = right_matrix([parts[0]] * 7, power(c2, 7) * power(c3, 4))
    set_phases(odd, re_sign, im_sign, ROWS, 7, False)
    angle = angle_ref[0:1]
    elsewhere = device_bits()

    @pl.loop(0, steps)
    def _(i):
        level_copy(i).wait()
        wave_copy(i).wait()
        for j in range(per):
            b = i * per + j
            k = (elsewhere + count_bits(b, 4)) & 3
            level = out_ref[pl.ds(b * 8, 8), pl.ds(2 * CHUNK, CHUNK)].reshape(ROWS, LANES)
            co, si = cos_sin(level * angle)
            re, im = wave[i, 0, j], wave[i, 1, j]
            swap = odd[k] > 0.5
            u = jnp.where(swap, im, re) * re_sign[k]
            v = jnp.where(swap, re, im) * im_sign[k]
            re, im = mix_rows_lanes(u * co + v * si, v * co - u * si, left[...], right[...])
            out_ref[pl.ds(b * 8, 8), pl.ds(0, CHUNK)] = re.reshape(8, CHUNK, LANES)
            out_ref[pl.ds(b * 8, 8), pl.ds(CHUNK, CHUNK)] = im.reshape(8, CHUNK, LANES)

    t2 = jnp.broadcast_to(s2 / c2, (8, LANES))

    @pl.loop(0, 32)
    def _(i):
        at, tile = i // 4, pl.ds(pl.multiple_of((i % 4) * 8, 8), 8)
        values = [out_ref[b * 8 + at, tile] for b in range(BLOCKS)]
        for b, value in enumerate(butterflies(values, [t2] * 4)):
            out_ref[b * 8 + at, tile] = value


def middle_kernel(turn_ref, angle_ref, in_ref, out_ref, held, left, right):
    before, after = angle_parts(turn_ref, 0), angle_parts(turn_ref, 1)
    (c0, s0), (c1, s1), (c2, s2), (c3, s3) = after
    left[...] = left_matrix([after[3]] * 3 + [after[1]] * 4, jnp.ones_like(c1))
    right[...] = right_matrix([after[0]] * 7, power(c2, 7) * c3 * power(c1, 3))
    angle = jnp.broadcast_to(angle_ref[1:2], (8, LANES))
    t2, t3 = (jnp.broadcast_to(before[g][1] / before[g][0], (8, LANES)) for g in (2, 3))

    @pl.loop(0, 32)
    def _(i):
        at, tile = i // 4, pl.ds(pl.multiple_of((i % 4) * 8, 8), 8)
        values = [in_ref[at * 16 + low, tile] for low in range(16)]
        for low, value in enumerate(butterflies(values, [t3] * 4)):
            held[at * 16 + low, tile] = value

    @pl.loop(0, 32)
    def _(i):
        low, row = i // 2, pl.multiple_of((i % 2) * 8, 8)
        re = butterflies([held[h * 16 + low, pl.ds(row, 8)] for h in range(8)], [t2] * 3)
        im = butterflies([held[h * 16 + low, pl.ds(CHUNK + row, 8)] for h in range(8)], [t2] * 3)
        for h in range(8):
            co, si = cos_sin(in_ref[h * 16 + low, pl.ds(2 * CHUNK + row, 8)] * angle)
            held[h * 16 + low, pl.ds(row, 8)] = re[h] * co + im[h] * si
            held[h * 16 + low, pl.ds(CHUNK + row, 8)] = im[h] * co - re[h] * si

    @pl.loop(0, 8)
    def _(i):
        for j in range(2):
            at = pl.ds((i * 2 + j) * 8, 8)
            re = held[at, pl.ds(0, CHUNK)].reshape(128, LANES)
            im = held[at, pl.ds(CHUNK, CHUNK)].reshape(128, LANES)
            re, im = mix_rows_lanes(re, im, left[...], right[...])
            held[at, pl.ds(0, CHUNK)] = re.reshape(8, CHUNK, LANES)
            held[at, pl.ds(CHUNK, CHUNK)] = im.reshape(8, CHUNK, LANES)

    u2, u3 = (jnp.broadcast_to(after[g][1] / after[g][0], (8, LANES)) for g in (2, 3))

    @pl.loop(0, 32)
    def _(i):
        at, tile = i // 4, pl.ds(pl.multiple_of((i % 4) * 8, 8), 8)
        values = [held[k * 8 + at, tile] for k in range(16)]
        for k, value in enumerate(butterflies(values, [u2] * 3 + [u3])):
            out_ref[k * 8 + at, tile] = value


def last_kernel(turn_ref, in_ref, out_ref, held, done, odd, re_sign, im_sign, sem):
    parts = angle_parts(turn_ref, 1)
    t1, t2 = (jnp.broadcast_to(parts[g][1] / parts[g][0], (8, LANES)) for g in (1, 2))
    set_phases(odd, re_sign, im_sign, CHUNK, 4, True)
    elsewhere = device_bits()

    @pl.loop(0, 32)
    def _(i):
        at, tile = i // 4, pl.ds(pl.multiple_of((i % 4) * 8, 8), 8)
        values = [in_ref[b * 8 + at, tile] for b in range(BLOCKS)]
        for b, value in enumerate(butterflies(values, [t2] * 4)):
            held[b * 8 + at, tile] = value

    def out_copy(b):
        return pltpu.make_async_copy(done.at[:, b], out_ref.at[:, b], sem.at[b])

    @pl.loop(0, BLOCKS)
    def _(b):
        base = elsewhere + count_bits(b, 4)
        for row in (0, 8):
            re = butterflies([held[b * 8 + r, pl.ds(row, 8)] for r in range(8)], [t1] * 3)
            im = butterflies([held[b * 8 + r, pl.ds(CHUNK + row, 8)] for r in range(8)], [t1] * 3)
            for r in range(8):
                k = (base + r.bit_count()) & 3
                swap = odd[k, pl.ds(row, 8)] > 0.5
                to = pl.ds(r * CHUNK + row, 8)
                done[0, b, to] = jnp.where(swap, im[r], re[r]) * re_sign[k, pl.ds(row, 8)]
                done[1, b, to] = jnp.where(swap, re[r], im[r]) * im_sign[k, pl.ds(row, 8)]
        out_copy(b).start()

    @pl.loop(0, BLOCKS)
    def _(b):
        out_copy(b).wait()


LIMIT = pltpu.CompilerParams(vmem_limit_bytes=20 << 20)


def spec(space):
    return pl.BlockSpec(memory_space=space)


def on_device(wave_parts, level_table, diagonal_angles, turn_angles):
    smem, vmem, hbm = spec(pltpu.SMEM), spec(pltpu.VMEM), spec(pltpu.HBM)
    phases = [pltpu.VMEM((4, ROWS, LANES), F32)] * 3
    sent = pl.pallas_call(
        first_kernel,
        name="first",
        compiler_params=LIMIT,
        out_shape=jax.ShapeDtypeStruct((DEVICES, 3 * CHUNK, LANES), F32),
        in_specs=[smem, vmem, hbm, hbm],
        out_specs=vmem,
        scratch_shapes=[
            pltpu.VMEM((8, 2, 2, ROWS, LANES), F32),
            pltpu.VMEM((256, 256), BF16),
            pltpu.VMEM((256, 256), BF16),
            *phases,
            pltpu.SemaphoreType.DMA((8,)),
            pltpu.SemaphoreType.DMA((8,)),
        ],
    )(turn_angles, diagonal_angles, wave_parts, level_table.reshape(DEVICES, CHUNK, LANES))
    held = lax.all_to_all(sent, HIGH_LOW, 0, 0, tiled=True)
    sent = pl.pallas_call(
        middle_kernel,
        name="middle",
        compiler_params=LIMIT,
        out_shape=jax.ShapeDtypeStruct((DEVICES, 2 * CHUNK, LANES), F32),
        in_specs=[smem, vmem, vmem],
        out_specs=vmem,
        scratch_shapes=[
            pltpu.VMEM((DEVICES, 2 * CHUNK, LANES), F32),
            pltpu.VMEM((256, 256), BF16),
            pltpu.VMEM((256, 256), BF16),
        ],
    )(turn_angles, diagonal_angles, held)
    held = lax.all_to_all(sent, HIGH_LOW, 0, 0, tiled=True)
    phases = [pltpu.VMEM((4, CHUNK, LANES), F32)] * 3
    return pl.pallas_call(
        last_kernel,
        name="last",
        compiler_params=LIMIT,
        out_shape=jax.ShapeDtypeStruct((2, BLOCKS, ROWS, LANES), F32),
        in_specs=[smem, vmem],
        out_specs=hbm,
        scratch_shapes=[
            pltpu.VMEM((DEVICES, 2 * CHUNK, LANES), F32),
            pltpu.VMEM((2, BLOCKS, ROWS, LANES), F32),
            *phases,
            pltpu.SemaphoreType.DMA((BLOCKS,)),
        ],
    )(turn_angles, held)


def solution(mesh):
    placed = (P(None, HIGH_LOW, None, None), P(HIGH_LOW, None, None), P(), P())
    return jax.shard_map(
        on_device,
        mesh=mesh,
        in_specs=placed,
        out_specs=P(None, HIGH_LOW, None, None),
        check_vma=False,
    )
```

profile of v0, /device:TPU:0, one launch (start us, length us, event | category | flops | bytes accessed | tf_op | source)
XLA Modules:
  0.0 108.1 jit_solution(6084412272928915227)
XLA Ops:
  0.0 0.0 copy-start
  0.0 1.6 %copy-done = f32[2,16,128,128]{3,2,1,0:T(8,128)S(1)} copy-done((f32[2,16,128,128]{3,2,1,0:T(8,128)S(1)}, f32[2,16,128,128]{3,2,1,0:T(8,128)}, u32[]{:S(2)}) %copy-start) | copy-done | bytes 2097176
  1.6 0.0 copy-start.1
  1.6 1.2 %copy-done.1 = f32[16,128,128]{2,1,0:T(8,128)S(1)} copy-done((f32[16,128,128]{2,1,0:T(8,128)S(1)}, f32[16,128,128]{2,1,0:T(8,128)}, u32[]{:S(2)}) %copy-start.1) | copy-done | bytes 1048600
  2.8 0.0 copy-start.2
  2.8 0.7 copy-done.2
  3.5 0.0 copy-start.3
  3.5 0.7 copy-done.3
  4.2 6.6 %first.1 = f32[128,48,128]{2,1,0:T(8,128)S(1)} custom-call(f32[2,4]{1,0:T(2,128)S(1)} %copy-done.2, f32[2,128]{1,0:T(2,128)S(1)} %copy-done.3, f32[2,16,128,128]{3,2,1,0:T(8,128)S(1)} %copy-done, f32[128,16,128]{2,1,0:T(8,128)S(1)} %bitcast.1), custom_call_target="tpu_custom_call" | custom-call | tf_op jit(solution)/shard_map/first/pallas_call | solution.py:278
  10.8 51.4 %all_to_all.10.in_ref = f32[128,48,128]{2,1,0:T(8,128)S(1)} all-to-all(f32[128,48,128]{2,1,0:T(8,128)S(1)} %first.1), channel_id=1, replica_groups=mesh['high'=8,'low'=16] {'high','low'}, dimensions={0} | all-to-all | bytes 6291456 | tf_op jit(solution)/shard_map/all_to_all | solution.py:294
  62.2 8.1 %middle.1 = f32[128,32,128]{2,1,0:T(8,128)S(1)} custom-call(f32[2,4]{1,0:T(2,128)S(1)} %copy-done.2, f32[2,128]{1,0:T(2,128)S(1)} %copy-done.3, f32[128,48,128]{2,1,0:T(8,128)S(1)} %all_to_all.10.in_ref), custom_call_target="tpu_custom_call" | custom-call | tf_op jit(solution)/shard_map/middle/pallas_call | solution.py:295
  70.3 34.7 %all_to_all.11.in_ref = f32[128,32,128]{2,1,0:T(8,128)S(1)} all-to-all(f32[128,32,128]{2,1,0:T(8,128)S(1)} %middle.1), channel_id=1, replica_groups=mesh['high'=8,'low'=16] {'high','low'}, dimensions={0} | all-to-all | bytes 4194304 | tf_op jit(solution)/shard_map/all_to_all | solution.py:308
  105.0 3.1 %last.1 = f32[2,16,128,128]{3,2,1,0:T(8,128)} custom-call(f32[2,4]{1,0:T(2,128)S(1)} %copy-done.2, f32[128,32,128]{2,1,0:T(8,128)S(1)} %all_to_all.11.in_ref), custom_call_target="tpu_custom_call" | custom-call | tf_op jit(solution)/shard_map/last/pallas_call | solution.py:310
Async XLA Ops:
  0.0 1.6 %copy-start = (f32[2,16,128,128]{3,2,1,0:T(8,128)S(1)}, f32[2,16,128,128]{3,2,1,0:T(8,128)}, u32[]{:S(2)}) copy-start(f32[2,16,128,128]{3,2,1,0:T(8,128)} %wave_ref.1) | copy-start | bytes 6291460
  1.6 1.2 %copy-start.1 = (f32[16,128,128]{2,1,0:T(8,128)S(1)}, f32[16,128,128]{2,1,0:T(8,128)}, u32[]{:S(2)}) copy-start(f32[16,128,128]{2,1,0:T(8,128)} %param.5) | copy-start | bytes 3145732
  2.8 0.7 copy-start.2
  3.5 0.7 copy-start.3
where the time goes:
time: 108 us
  blocking collectives  86.1 us (80%)
  Pallas kernels  17.8 us (16%)
  local copies, waits for them, and re-layouts  4.17 us (4%)
    all_to_all x2, blocking collectives, on_device(): held = lax.all_to_all(sent, HIGH_LOW, 0, 0, tiled=True)  86.1 us
    pallas_call x1, Pallas kernels, on_device(): pl.pallas_call(middle_kernel, name='middle', compiler_params=LIMIT, out_s...  8.12 us
    pallas_call x1, Pallas kernels, on_device(): pl.pallas_call(first_kernel, name='first', compiler_params=LIMIT, out_sha...  6.6 us
    unnamed x8, local copies, waits for them, and re-layouts  4.17 us
    pallas_call x1, Pallas kernels, on_device(): pl.pallas_call(last_kernel, name='last', compiler_params=LIMIT, out_shape...  3.11 us

commit v1 on v0

--- a/solution.py
+++ b/solution.py
@@ -10,6 +10,8 @@
 BLOCKS = 16
 ROWS = 128
 LANES = 128
+LOWS = 8
+STEPS = 2
 CHUNK = 16
 F32 = jnp.float32
 BF16 = jnp.bfloat16
@@ -113,6 +115,17 @@
     return total
 
 
+def mix_major(take, put, place, tangents):
+    @pl.loop(0, 16)
+    def _(i):
+        at = i // 2
+        for j in range(2):
+            tile = pl.ds(pl.multiple_of((i % 2) * 16, 16) + j * 8, 8)
+            values = [take[place(k, at), tile] for k in range(16)]
+            for k, value in enumerate(butterflies(values, tangents)):
+                put[place(k, at), tile] = value
+
+
 def device_bits():
     return count_bits(lax.axis_index("high"), 3) + count_bits(lax.axis_index("low"), 4)
 
@@ -129,9 +142,9 @@
         im_sign_ref[k] = plus if back else minus
 
 
-def first_kernel(turn_ref, angle_ref, wave_ref, level_ref, out_ref, wave, left, right,
-                 odd, re_sign, im_sign, wave_sem, level_sem):
-    steps = 8
+def first_kernel(turn_hbm, angle_hbm, wave_ref, level_ref, out_ref, turn_ref, angle_ref, wave, left, right,
+                 odd, re_sign, im_sign, small_sem, wave_sem, level_sem):
+    steps = STEPS
     per = BLOCKS // steps
 
     def wave_copy(i):
@@ -146,15 +159,21 @@
             level_sem.at[i],
         )
 
+    turn_copy = pltpu.make_async_copy(turn_hbm, turn_ref, small_sem.at[0])
+    angle_copy = pltpu.make_async_copy(angle_hbm, angle_ref, small_sem.at[1])
+    turn_copy.start()
+    angle_copy.start()
     for i in range(steps):
         level_copy(i).start()
         wave_copy(i).start()
 
+    set_phases(odd, re_sign, im_sign, ROWS, 7, False)
+    turn_copy.wait()
+    angle_copy.wait()
     parts = angle_parts(turn_ref, 0)
     (c0, s0), (c1, s1), (c2, s2), (c3, s3) = parts
     left[...] = left_matrix([parts[1]] * 7, jnp.ones_like(c1))
     right[...] = right_matrix([parts[0]] * 7, power(c2, 7) * power(c3, 4))
-    set_phases(odd, re_sign, im_sign, ROWS, 7, False)
     angle = angle_ref[0:1]
     elsewhere = device_bits()
 
@@ -177,57 +196,38 @@
 
     t2 = jnp.broadcast_to(s2 / c2, (8, LANES))
 
-    @pl.loop(0, 32)
-    def _(i):
-        at, tile = i // 4, pl.ds(pl.multiple_of((i % 4) * 8, 8), 8)
-        values = [out_ref[b * 8 + at, tile] for b in range(BLOCKS)]
-        for b, value in enumerate(butterflies(values, [t2] * 4)):
-            out_ref[b * 8 + at, tile] = value
+    mix_major(out_ref, out_ref, lambda k, at: k * 8 + at, [t2] * 4)
 
 
 def middle_kernel(turn_ref, angle_ref, in_ref, out_ref, held, left, right):
     before, after = angle_parts(turn_ref, 0), angle_parts(turn_ref, 1)
     (c0, s0), (c1, s1), (c2, s2), (c3, s3) = after
-    left[...] = left_matrix([after[3]] * 3 + [after[1]] * 4, jnp.ones_like(c1))
-    right[...] = right_matrix([after[0]] * 7, power(c2, 7) * c3 * power(c1, 3))
-    angle = jnp.broadcast_to(angle_ref[1:2], (8, LANES))
-    t2, t3 = (jnp.broadcast_to(before[g][1] / before[g][0], (8, LANES)) for g in (2, 3))
-
-    @pl.loop(0, 32)
+    left[...] = left_matrix([after[2]] * 3 + [after[1]] * 4, jnp.ones_like(c1))
+    right[...] = right_matrix([after[0]] * 7, power(c3, 4) * power(c2, 4) * power(c1, 3))
+    angle = angle_ref[1:2]
+    t2, t3 = (before[g][1] / before[g][0] for g in (2, 3))
+
+    mix_major(in_ref, held, lambda k, at: at * 16 + k, [jnp.broadcast_to(t3, (8, LANES))] * 4)
+
+    @pl.loop(0, 16 // LOWS)
     def _(i):
-        at, tile = i // 4, pl.ds(pl.multiple_of((i % 4) * 8, 8), 8)
-        values = [in_ref[at * 16 + low, tile] for low in range(16)]
-        for low, value in enumerate(butterflies(values, [t3] * 4)):
-            held[at * 16 + low, tile] = value
-
-    @pl.loop(0, 32)
-    def _(i):
-        low, row = i // 2, pl.multiple_of((i % 2) * 8, 8)
-        re = butterflies([held[h * 16 + low, pl.ds(row, 8)] for h in range(8)], [t2] * 3)
-        im = butterflies([held[h * 16 + low, pl.ds(CHUNK + row, 8)] for h in range(8)], [t2] * 3)
-        for h in range(8):
-            co, si = cos_sin(in_ref[h * 16 + low, pl.ds(2 * CHUNK + row, 8)] * angle)
-            held[h * 16 + low, pl.ds(row, 8)] = re[h] * co + im[h] * si
-            held[h * 16 + low, pl.ds(CHUNK + row, 8)] = im[h] * co - re[h] * si
-
-    @pl.loop(0, 8)
-    def _(i):
-        for j in range(2):
-            at = pl.ds((i * 2 + j) * 8, 8)
-            re = held[at, pl.ds(0, CHUNK)].reshape(128, LANES)
-            im = held[at, pl.ds(CHUNK, CHUNK)].reshape(128, LANES)
+        for j in range(LOWS):
+            low = i * LOWS + j
+            at = [h * 16 + low for h in range(8)]
+            re = butterflies([held[k, pl.ds(0, CHUNK)] for k in at], [t2] * 3)
+            im = butterflies([held[k, pl.ds(CHUNK, CHUNK)] for k in at], [t2] * 3)
+            turned = []
+            for h in range(8):
+                co, si = cos_sin(in_ref[at[h], pl.ds(2 * CHUNK, CHUNK)] * angle)
+                turned.append((re[h] * co + im[h] * si, im[h] * co - re[h] * si))
+            re, im = (jnp.concatenate(part, 0) for part in zip(*turned))
             re, im = mix_rows_lanes(re, im, left[...], right[...])
-            held[at, pl.ds(0, CHUNK)] = re.reshape(8, CHUNK, LANES)
-            held[at, pl.ds(CHUNK, CHUNK)] = im.reshape(8, CHUNK, LANES)
-
-    u2, u3 = (jnp.broadcast_to(after[g][1] / after[g][0], (8, LANES)) for g in (2, 3))
-
-    @pl.loop(0, 32)
-    def _(i):
-        at, tile = i // 4, pl.ds(pl.multiple_of((i % 4) * 8, 8), 8)
-        values = [held[k * 8 + at, tile] for k in range(16)]
-        for k, value in enumerate(butterflies(values, [u2] * 3 + [u3])):
-            out_ref[k * 8 + at, tile] = value
+            for h in range(8):
+                held[at[h], pl.ds(0, CHUNK)] = re[h * CHUNK : (h + 1) * CHUNK]
+                held[at[h], pl.ds(CHUNK, CHUNK)] = im[h * CHUNK : (h + 1) * CHUNK]
+
+    u3 = jnp.broadcast_to(s3 / c3, (8, LANES))
+    mix_major(held, out_ref, lambda k, at: at * 16 + k, [u3] * 4)
 
 
 def last_kernel(turn_ref, in_ref, out_ref, held, done, odd, re_sign, im_sign, sem):
@@ -236,12 +236,7 @@
     set_phases(odd, re_sign, im_sign, CHUNK, 4, True)
     elsewhere = device_bits()
 
-    @pl.loop(0, 32)
-    def _(i):
-        at, tile = i // 4, pl.ds(pl.multiple_of((i % 4) * 8, 8), 8)
-        values = [in_ref[b * 8 + at, tile] for b in range(BLOCKS)]
-        for b, value in enumerate(butterflies(values, [t2] * 4)):
-            held[b * 8 + at, tile] = value
+    mix_major(in_ref, held, lambda k, at: k * 8 + at, [t2] * 4)
 
     def out_copy(b):
         return pltpu.make_async_copy(done.at[:, b], out_ref.at[:, b], sem.at[b])
@@ -280,17 +275,30 @@
         name="first",
         compiler_params=LIMIT,
         out_shape=jax.ShapeDtypeStruct((DEVICES, 3 * CHUNK, LANES), F32),
-        in_specs=[smem, vmem, hbm, hbm],
+        in_specs=[hbm] * 4,
         out_specs=vmem,
         scratch_shapes=[
-            pltpu.VMEM((8, 2, 2, ROWS, LANES), F32),
+            pltpu.SMEM((2, 4), F32),
+            pltpu.VMEM((2, LANES), F32),
+            pltpu.VMEM((STEPS, 2, BLOCKS // STEPS, ROWS, LANES), F32),
             pltpu.VMEM((256, 256), BF16),
             pltpu.VMEM((256, 256), BF16),
             *phases,
-            pltpu.SemaphoreType.DMA((8,)),
-            pltpu.SemaphoreType.DMA((8,)),
+            pltpu.SemaphoreType.DMA((2,)),
+            pltpu.SemaphoreType.DMA((STEPS,)),
+            pltpu.SemaphoreType.DMA((STEPS,)),
         ],
-    )(turn_angles, diagonal_angles, wave_parts, level_table.reshape(DEVICES, CHUNK, LANES))
+    )(
+        *(
+            pltpu.with_memory_space_constraint(x, pltpu.HBM)
+            for x in (
+                turn_angles,
+                diagonal_angles,
+                wave_parts,
+                level_table.reshape(DEVICES, CHUNK, LANES),
+            )
+        )
+    )
     held = lax.all_to_all(sent, HIGH_LOW, 0, 0, tiled=True)
     sent = pl.pallas_call(
         middle_kernel,

time: 108 us -> 98.7 us (0.914)
  Pallas kernels: 17.8 us -> 12.4 us
  local copies, waits for them, and re-layouts: 4.17 us -> 0.01 us
    unnamed x8 -> x4, local copies, waits for them, and re-layouts: 4.17 us -> 0.01 us
    pallas_call x1, Pallas kernels: 8.12 us -> 4.9 us  [on_device(): pl.pallas_call(middle_kernel, name='middle', compiler_params=LIMIT, out_s...]
    pallas_call x1, Pallas kernels: 6.6 us -> 4.64 us  [on_device(): pl.pallas_call(first_kernel, name='first', compiler_params=LIMIT, out_sha...]
where the time goes in v1:
time: 98.7 us; the launch traced here: 98.6 us
  blocking collectives  86.1 us (87%)
  Pallas kernels  12.4 us (13%)
    all_to_all x2, blocking collectives, on_device(): held = lax.all_to_all(sent, HIGH_LOW, 0, 0, tiled=True)  86.1 us
    pallas_call x1, Pallas kernels, on_device(): pl.pallas_call(middle_kernel, name='middle', compiler_params=LIMIT, out_s...  4.9 us
    pallas_call x1, Pallas kernels, on_device(): pl.pallas_call(first_kernel, name='first', compiler_params=LIMIT, out_sha...  4.64 us
    pallas_call x1, Pallas kernels, on_device(): pl.pallas_call(last_kernel, name='last', compiler_params=LIMIT, out_shape...  2.88 us

profile of v1, /device:TPU:0, one launch (start us, length us, event | category | flops | bytes accessed | tf_op | source)
XLA Modules:
  0.0 98.6 jit_solution(1777129819273941735)
XLA Ops:
  0.0 4.6 %first.1 = f32[128,48,128]{2,1,0:T(8,128)S(1)} custom-call(f32[2,4]{1,0:T(2,128)} %turn_ref.3, f32[2,128]{1,0:T(2,128)} %angle_ref.1, f32[2,16,128,128]{3,2,1,0:T(8,128)} %wave_ref.1, f32[128,16,128]{2,1,0:T(8,128)} %bitcast.1), custom_call_target="tpu_custom_call" | custom-call | tf_op jit(solution)/shard_map/first/pallas_call | solution.py:273
  4.7 0.0 copy-start
  4.7 0.0 copy-start.1
  4.7 51.4 %all_to_all.10.in_ref = f32[128,48,128]{2,1,0:T(8,128)S(1)} all-to-all(f32[128,48,128]{2,1,0:T(8,128)S(1)} %first.1), channel_id=1, replica_groups=mesh['high'=8,'low'=16] {'high','low'}, dimensions={0} | all-to-all | bytes 6291456 | tf_op jit(solution)/shard_map/all_to_all | solution.py:302
  56.0 0.0 copy-done
  56.0 0.0 copy-done.1
  56.1 4.9 %middle.1 = f32[128,32,128]{2,1,0:T(8,128)S(1)} custom-call(f32[2,4]{1,0:T(2,128)S(1)} %copy-done, f32[2,128]{1,0:T(2,128)S(1)} %copy-done.1, f32[128,48,128]{2,1,0:T(8,128)S(1)} %all_to_all.10.in_ref), custom_call_target="tpu_custom_call" | custom-call | tf_op jit(solution)/shard_map/middle/pallas_call | solution.py:303
  61.0 34.7 %all_to_all.11.in_ref = f32[128,32,128]{2,1,0:T(8,128)S(1)} all-to-all(f32[128,32,128]{2,1,0:T(8,128)S(1)} %middle.1), channel_id=1, replica_groups=mesh['high'=8,'low'=16] {'high','low'}, dimensions={0} | all-to-all | bytes 4194304 | tf_op jit(solution)/shard_map/all_to_all | solution.py:316
  95.7 2.9 %last.1 = f32[2,16,128,128]{3,2,1,0:T(8,128)} custom-call(f32[2,4]{1,0:T(2,128)S(1)} %copy-done, f32[128,32,128]{2,1,0:T(8,128)S(1)} %all_to_all.11.in_ref), custom_call_target="tpu_custom_call" | custom-call | tf_op jit(solution)/shard_map/last/pallas_call | solution.py:318
Async XLA Ops:
  4.7 51.4 %copy-start = (f32[2,4]{1,0:T(2,128)S(1)}, f32[2,4]{1,0:T(2,128)}, u32[]{:S(2)}) copy-start(f32[2,4]{1,0:T(2,128)} %turn_ref.3) | copy-start | bytes 100
  4.7 51.4 %copy-start.1 = (f32[2,128]{1,0:T(2,128)S(1)}, f32[2,128]{1,0:T(2,128)}, u32[]{:S(2)}) copy-start(f32[2,128]{1,0:T(2,128)} %angle_ref.1) | copy-start | bytes 3076

commit v2 on v1

--- a/solution.py
+++ b/solution.py
@@ -10,7 +10,7 @@
 BLOCKS = 16
 ROWS = 128
 LANES = 128
-LOWS = 8
+LOWS = 16
 STEPS = 2
 CHUNK = 16
 F32 = jnp.float32
@@ -116,11 +116,10 @@
 
 
 def mix_major(take, put, place, tangents):
-    @pl.loop(0, 16)
-    def _(i):
-        at = i // 2
-        for j in range(2):
-            tile = pl.ds(pl.multiple_of((i % 2) * 16, 16) + j * 8, 8)
+    @pl.loop(0, 8)
+    def _(at):
+        for row in range(0, 32, 8):
+            tile = pl.ds(row, 8)
             values = [take[place(k, at), tile] for k in range(16)]
             for k, value in enumerate(butterflies(values, tangents)):
                 put[place(k, at), tile] = value
@@ -142,7 +141,16 @@
         im_sign_ref[k] = plus if back else minus
 
 
-def first_kernel(turn_hbm, angle_hbm, wave_ref, level_ref, out_ref, turn_ref, angle_ref, wave, left, right,
+def later_tables(before, after, angle_ref, left, right, rows):
+    (c0, s0), (c1, s1), (c2, s2), (c3, s3) = after
+    left[...] = left_matrix([after[2]] * 3 + [after[1]] * 4, jnp.ones_like(c1))
+    right[...] = right_matrix([after[0]] * 7, power(c3, 4) * power(c2, 4) * power(c1, 3))
+    made = [before[2][1] / before[2][0], before[3][1] / before[3][0], s1 / c1, s2 / c2, s3 / c3]
+    for k, row in enumerate([*made, angle_ref[1:2]]):
+        rows[k] = jnp.broadcast_to(row, (8, LANES))
+
+
+def first_kernel(turn_hbm, angle_hbm, wave_ref, level_ref, out_ref, later_left, later_right, later_rows, turn_ref, angle_ref, wave, left, right,
                  odd, re_sign, im_sign, small_sem, wave_sem, level_sem):
     steps = STEPS
     per = BLOCKS // steps
@@ -174,6 +182,7 @@
     (c0, s0), (c1, s1), (c2, s2), (c3, s3) = parts
     left[...] = left_matrix([parts[1]] * 7, jnp.ones_like(c1))
     right[...] = right_matrix([parts[0]] * 7, power(c2, 7) * power(c3, 4))
+    later_tables(parts, angle_parts(turn_ref, 1), angle_ref, later_left, later_right, later_rows)
     angle = angle_ref[0:1]
     elsewhere = device_bits()
 
@@ -199,15 +208,9 @@
     mix_major(out_ref, out_ref, lambda k, at: k * 8 + at, [t2] * 4)
 
 
-def middle_kernel(turn_ref, angle_ref, in_ref, out_ref, held, left, right):
-    before, after = angle_parts(turn_ref, 0), angle_parts(turn_ref, 1)
-    (c0, s0), (c1, s1), (c2, s2), (c3, s3) = after
-    left[...] = left_matrix([after[2]] * 3 + [after[1]] * 4, jnp.ones_like(c1))
-    right[...] = right_matrix([after[0]] * 7, power(c3, 4) * power(c2, 4) * power(c1, 3))
-    angle = angle_ref[1:2]
-    t2, t3 = (before[g][1] / before[g][0] for g in (2, 3))
-
-    mix_major(in_ref, held, lambda k, at: at * 16 + k, [jnp.broadcast_to(t3, (8, LANES))] * 4)
+def middle_kernel(rows, left, right, in_ref, out_ref, held):
+    angle, t2 = rows[5, 0:1], rows[0, 0:1]
+    mix_major(in_ref, held, lambda k, at: at * 16 + k, [rows[1]] * 4)
 
     @pl.loop(0, 16 // LOWS)
     def _(i):
@@ -226,38 +229,51 @@
                 held[at[h], pl.ds(0, CHUNK)] = re[h * CHUNK : (h + 1) * CHUNK]
                 held[at[h], pl.ds(CHUNK, CHUNK)] = im[h * CHUNK : (h + 1) * CHUNK]
 
-    u3 = jnp.broadcast_to(s3 / c3, (8, LANES))
-    mix_major(held, out_ref, lambda k, at: at * 16 + k, [u3] * 4)
-
-
-def last_kernel(turn_ref, in_ref, out_ref, held, done, odd, re_sign, im_sign, sem):
-    parts = angle_parts(turn_ref, 1)
-    t1, t2 = (jnp.broadcast_to(parts[g][1] / parts[g][0], (8, LANES)) for g in (1, 2))
+    mix_major(held, out_ref, lambda k, at: at * 16 + k, [rows[4]] * 4)
+
+
+def last_kernel(rows, in_ref, out_ref, held, done, odd, re_sign, im_sign, sem):
+    t1, t2 = rows[2], rows[3]
     set_phases(odd, re_sign, im_sign, CHUNK, 4, True)
     elsewhere = device_bits()
 
-    mix_major(in_ref, held, lambda k, at: k * 8 + at, [t2] * 4)
-
-    def out_copy(b):
-        return pltpu.make_async_copy(done.at[:, b], out_ref.at[:, b], sem.at[b])
-
-    @pl.loop(0, BLOCKS)
-    def _(b):
-        base = elsewhere + count_bits(b, 4)
-        for row in (0, 8):
-            re = butterflies([held[b * 8 + r, pl.ds(row, 8)] for r in range(8)], [t1] * 3)
-            im = butterflies([held[b * 8 + r, pl.ds(CHUNK + row, 8)] for r in range(8)], [t1] * 3)
-            for r in range(8):
-                k = (base + r.bit_count()) & 3
-                swap = odd[k, pl.ds(row, 8)] > 0.5
-                to = pl.ds(r * CHUNK + row, 8)
-                done[0, b, to] = jnp.where(swap, im[r], re[r]) * re_sign[k, pl.ds(row, 8)]
-                done[1, b, to] = jnp.where(swap, re[r], im[r]) * im_sign[k, pl.ds(row, 8)]
-        out_copy(b).start()
-
-    @pl.loop(0, BLOCKS)
-    def _(b):
-        out_copy(b).wait()
+    def out_copy(half, b):
+        return pltpu.make_async_copy(
+            done.at[:, b, :, half], out_ref.at[:, b, :, half], sem.at[half, b]
+        )
+
+    for half in range(2):
+        re_rows, im_rows = pl.ds(half * 8, 8), pl.ds(CHUNK + half * 8, 8)
+
+        @pl.loop(0, 4)
+        def _(i):
+            for j in range(2):
+                for tile in (re_rows, im_rows):
+                    at = i * 2 + j
+                    values = [in_ref[b * 8 + at, tile] for b in range(BLOCKS)]
+                    for b, value in enumerate(butterflies(values, [t2] * 4)):
+                        held[b * 8 + at, tile] = value
+
+        @pl.loop(0, BLOCKS // 2)
+        def _(i):
+            for j in range(2):
+                b = i * 2 + j
+                base = elsewhere + count_bits(b, 4)
+                re = butterflies([held[b * 8 + r, re_rows] for r in range(8)], [t1] * 3)
+                im = butterflies([held[b * 8 + r, im_rows] for r in range(8)], [t1] * 3)
+                for r in range(8):
+                    k = (base + r.bit_count()) & 3
+                    swap = odd[k, re_rows] > 0.5
+                    done[0, b, r, half] = jnp.where(swap, im[r], re[r]) * re_sign[k, re_rows]
+                    done[1, b, r, half] = jnp.where(swap, re[r], im[r]) * im_sign[k, re_rows]
+            for j in range(2):
+                out_copy(half, i * 2 + j).start()
+
+    for half in range(2):
+
+        @pl.loop(0, BLOCKS)
+        def _(b):
+            out_copy(half, b).wait()
 
 
 LIMIT = pltpu.CompilerParams(vmem_limit_bytes=20 << 20)
@@ -268,22 +284,27 @@
 
 
 def on_device(wave_parts, level_table, diagonal_angles, turn_angles):
-    smem, vmem, hbm = spec(pltpu.SMEM), spec(pltpu.VMEM), spec(pltpu.HBM)
-    phases = [pltpu.VMEM((4, ROWS, LANES), F32)] * 3
-    sent = pl.pallas_call(
+    vmem, hbm = spec(pltpu.VMEM), spec(pltpu.HBM)
+    square = (256, 256)
+    sent, left, right, rows = pl.pallas_call(
         first_kernel,
         name="first",
         compiler_params=LIMIT,
-        out_shape=jax.ShapeDtypeStruct((DEVICES, 3 * CHUNK, LANES), F32),
+        out_shape=[
+            jax.ShapeDtypeStruct((DEVICES, 3 * CHUNK, LANES), F32),
+            jax.ShapeDtypeStruct(square, BF16),
+            jax.ShapeDtypeStruct(square, BF16),
+            jax.ShapeDtypeStruct((6, 8, LANES), F32),
+        ],
         in_specs=[hbm] * 4,
-        out_specs=vmem,
+        out_specs=[vmem] * 4,
         scratch_shapes=[
             pltpu.SMEM((2, 4), F32),
             pltpu.VMEM((2, LANES), F32),
             pltpu.VMEM((STEPS, 2, BLOCKS // STEPS, ROWS, LANES), F32),
-            pltpu.VMEM((256, 256), BF16),
-            pltpu.VMEM((256, 256), BF16),
-            *phases,
+            pltpu.VMEM(square, BF16),
+            pltpu.VMEM(square, BF16),
+            *[pltpu.VMEM((4, ROWS, LANES), F32)] * 3,
             pltpu.SemaphoreType.DMA((2,)),
             pltpu.SemaphoreType.DMA((STEPS,)),
             pltpu.SemaphoreType.DMA((STEPS,)),
@@ -305,30 +326,27 @@
         name="middle",
         compiler_params=LIMIT,
         out_shape=jax.ShapeDtypeStruct((DEVICES, 2 * CHUNK, LANES), F32),
-        in_specs=[smem, vmem, vmem],
+        in_specs=[vmem] * 4,
         out_specs=vmem,
-        scratch_shapes=[
-            pltpu.VMEM((DEVICES, 2 * CHUNK, LANES), F32),
-            pltpu.VMEM((256, 256), BF16),
-            pltpu.VMEM((256, 256), BF16),
-        ],
-    )(turn_angles, diagonal_angles, held)
+        scratch_shapes=[pltpu.VMEM((DEVICES, 2 * CHUNK, LANES), F32)],
+    )(rows, left, right, held)
     held = lax.all_to_all(sent, HIGH_LOW, 0, 0, tiled=True)
-    phases = [pltpu.VMEM((4, CHUNK, LANES), F32)] * 3
-    return pl.pallas_call(
+    tiled = (2, BLOCKS, 8, 2, 8, LANES)
+    out = pl.pallas_call(
         last_kernel,
         name="last",
         compiler_params=LIMIT,
-        out_shape=jax.ShapeDtypeStruct((2, BLOCKS, ROWS, LANES), F32),
-        in_specs=[smem, vmem],
+        out_shape=jax.ShapeDtypeStruct(tiled, F32),
+        in_specs=[vmem] * 2,
         out_specs=hbm,
         scratch_shapes=[
             pltpu.VMEM((DEVICES, 2 * CHUNK, LANES), F32),
-            pltpu.VMEM((2, BLOCKS, ROWS, LANES), F32),
-            *phases,
-            pltpu.SemaphoreType.DMA((BLOCKS,)),
+            pltpu.VMEM(tiled, F32),
+            *[pltpu.VMEM((4, CHUNK, LANES), F32)] * 3,
+            pltpu.SemaphoreType.DMA((2, BLOCKS)),
         ],
-    )(turn_angles, held)
+    )(rows, held)
+    return out.reshape(2, BLOCKS, ROWS, LANES)
 
 
 def solution(mesh):

time: 98.7 us -> 96.8 us (0.981)
  Pallas kernels: 12.4 us -> 10.6 us
    pallas_call x1, Pallas kernels: 4.9 us -> 3.55 us  [on_device(): pl.pallas_call(middle_kernel, name='middle', compiler_params=LIMIT, out_s...]
where the time goes in v2:
time: 96.8 us; the launch traced here: 96.7 us
  blocking collectives  86.1 us (89%)
  Pallas kernels  10.6 us (11%)
    all_to_all x2, blocking collectives, on_device(): held = lax.all_to_all(sent, HIGH_LOW, 0, 0, tiled=True)  86.1 us
    pallas_call x1, Pallas kernels, on_device(): pl.pallas_call(first_kernel, name='first', compiler_params=LIMIT, out_sha...  4.62 us
    pallas_call x1, Pallas kernels, on_device(): pl.pallas_call(middle_kernel, name='middle', compiler_params=LIMIT, out_s...  3.55 us
    pallas_call x1, Pallas kernels, on_device(): pl.pallas_call(last_kernel, name='last', compiler_params=LIMIT, out_shape...  2.4 us

profile of v2, /device:TPU:0, one launch (start us, length us, event | category | flops | bytes accessed | tf_op | source)
XLA Modules:
  0.0 96.7 jit_solution(15658952195541726167)
XLA Ops:
  0.0 4.6 %first.1 = (f32[128,48,128]{2,1,0:T(8,128)S(1)}, bf16[256,256]{1,0:T(8,128)(2,1)S(1)}, bf16[256,256]{1,0:T(8,128)(2,1)S(1)}, f32[6,8,128]{2,1,0:T(8,128)S(1)}) custom-call(f32[2,4]{1,0:T(2,128)} %turn_hbm.1, f32[2,128]{1,0:T(2,128)} %angle_hbm.1, f32[2,16,128,128]{3,2,1,0:T(8,128)} %wave_ref.1, f32[128,16,128]{2,1,0:T(8,128)} %bitcast.2), custom_call_target="tpu_custom_call" | custom-call | tf_op jit(solution)/shard_map/first/pallas_call | solution.py:289
  4.6 51.4 %all_to_all.10.in_ref = f32[128,48,128]{2,1,0:T(8,128)S(1)} all-to-all(f32[128,48,128]{2,1,0:T(8,128)S(1)} %get-tuple-element.12), channel_id=1, replica_groups=mesh['high'=8,'low'=16] {'high','low'}, dimensions={0} | all-to-all | bytes 6291456 | tf_op jit(solution)/shard_map/all_to_all | solution.py:323
  56.0 3.5 %middle.1 = f32[128,32,128]{2,1,0:T(8,128)S(1)} custom-call(f32[6,8,128]{2,1,0:T(8,128)S(1)} %get-tuple-element.9.rows, bf16[256,256]{1,0:T(8,128)(2,1)S(1)} %get-tuple-element.10.left, bf16[256,256]{1,0:T(8,128)(2,1)S(1)} %get-tuple-element.11.right, f32[128,48,128]{2,1,0:T(8,128)S(1)} %all_to_all.10.in_ref), custom_call_target="tpu_custom_call" | custom-call | tf_op jit(solution)/shard_map/middle/pallas_call | solution.py:324
  59.6 34.7 %all_to_all.11.in_ref = f32[128,32,128]{2,1,0:T(8,128)S(1)} all-to-all(f32[128,32,128]{2,1,0:T(8,128)S(1)} %middle.1), channel_id=1, replica_groups=mesh['high'=8,'low'=16] {'high','low'}, dimensions={0} | all-to-all | bytes 4194304 | tf_op jit(solution)/shard_map/all_to_all | solution.py:333
  94.3 2.4 %last.1 = f32[2,16,8,2,8,128]{5,4,3,2,1,0:T(8,128)} custom-call(f32[6,8,128]{2,1,0:T(8,128)S(1)} %get-tuple-element.9.rows, f32[128,32,128]{2,1,0:T(8,128)S(1)} %all_to_all.11.in_ref), custom_call_target="tpu_custom_call" | custom-call | tf_op jit(solution)/shard_map/last/pallas_call | solution.py:335

commit v3 on v2

--- a/solution.py
+++ b/solution.py
@@ -11,7 +11,7 @@
 ROWS = 128
 LANES = 128
 LOWS = 16
-STEPS = 2
+STEPS = 1
 CHUNK = 16
 F32 = jnp.float32
 BF16 = jnp.bfloat16
@@ -115,13 +115,45 @@
     return total
 
 
-def mix_major(take, put, place, tangents):
+def turned(u, v, c, s):
+    return c * u + s * v, c * v - s * u
+
+
+def two_bits(u):
+    return u[1] + u[2], u[3] - u[0], u[0] + u[3], u[1] - u[2]
+
+
+def two_bits_back(p, m, q, n):
+    return q - m, p + n, p - n, q + m
+
+
+def double_angles(c, s):
+    c2, s2 = 1 - 2 * s * s, 2 * s * c
+    return c2, s2, 0.5 - s2 * s2, s2 * c2
+
+
+def mix_four(values, angles):
+    c2, s2, half_c4, half_s4 = angles
+    rows = [two_bits(values[i : i + 4]) for i in range(0, 16, 4)]
+    p, m, q, n = (list(two_bits(column)) for column in zip(*rows))
+    for part in (q, n):
+        part[0], part[1] = turned(part[0], part[1], c2, s2)
+    for k in (2, 3):
+        p[k], m[k] = turned(p[k], m[k], c2, s2)
+    pp, mm, qq, nn = two_bits((p[0], p[1], m[0], m[1]))
+    pp, mm = turned(pp, mm, half_c4, half_s4)
+    p[0], p[1], m[0], m[1] = two_bits_back(pp, mm, 0.5 * qq, 0.5 * nn)
+    columns = [two_bits_back(*part) for part in (p, m, q, n)]
+    return [u for row in zip(*columns) for u in two_bits_back(*row)]
+
+
+def mix_major(take, put, place, angles):
     @pl.loop(0, 8)
     def _(at):
         for row in range(0, 32, 8):
             tile = pl.ds(row, 8)
             values = [take[place(k, at), tile] for k in range(16)]
-            for k, value in enumerate(butterflies(values, tangents)):
+            for k, value in enumerate(mix_four(values, angles)):
                 put[place(k, at), tile] = value
 
 
@@ -144,14 +176,16 @@
 def later_tables(before, after, angle_ref, left, right, rows):
     (c0, s0), (c1, s1), (c2, s2), (c3, s3) = after
     left[...] = left_matrix([after[2]] * 3 + [after[1]] * 4, jnp.ones_like(c1))
-    right[...] = right_matrix([after[0]] * 7, power(c3, 4) * power(c2, 4) * power(c1, 3))
-    made = [before[2][1] / before[2][0], before[3][1] / before[3][0], s1 / c1, s2 / c2, s3 / c3]
-    for k, row in enumerate([*made, angle_ref[1:2]]):
+    right[...] = right_matrix([after[0]] * 7, power(c1, 3) / 16)
+    made = [angle_ref[1:2], before[2][1] / before[2][0], s1 / c1]
+    for c, s in (before[3], after[3], after[2]):
+        made.extend(double_angles(c, s))
+    for k, row in enumerate(made):
         rows[k] = jnp.broadcast_to(row, (8, LANES))
 
 
 def first_kernel(turn_hbm, angle_hbm, wave_ref, level_ref, out_ref, later_left, later_right, later_rows, turn_ref, angle_ref, wave, left, right,
-                 odd, re_sign, im_sign, small_sem, wave_sem, level_sem):
+                 levels, cosines, sines, odd, re_sign, im_sign, small_sem, wave_sem):
     steps = STEPS
     per = BLOCKS // steps
 
@@ -160,57 +194,58 @@
             wave_ref.at[:, pl.ds(i * per, per)], wave.at[i], wave_sem.at[i]
         )
 
-    def level_copy(i):
-        return pltpu.make_async_copy(
-            level_ref.at[pl.ds(i * per * 8, per * 8)],
-            out_ref.at[pl.ds(i * per * 8, per * 8), pl.ds(2 * CHUNK, CHUNK)],
-            level_sem.at[i],
-        )
-
+    level_copy = pltpu.make_async_copy(
+        level_ref, levels, small_sem.at[2]
+    )
     turn_copy = pltpu.make_async_copy(turn_hbm, turn_ref, small_sem.at[0])
     angle_copy = pltpu.make_async_copy(angle_hbm, angle_ref, small_sem.at[1])
     turn_copy.start()
     angle_copy.start()
-    for i in range(steps):
-        level_copy(i).start()
-        wave_copy(i).start()
-
-    set_phases(odd, re_sign, im_sign, ROWS, 7, False)
+    level_copy.start()
+    set_phases(odd, re_sign, im_sign, ROWS, 7, True)
+    wave_copy(0).start()
     turn_copy.wait()
     angle_copy.wait()
     parts = angle_parts(turn_ref, 0)
     (c0, s0), (c1, s1), (c2, s2), (c3, s3) = parts
     left[...] = left_matrix([parts[1]] * 7, jnp.ones_like(c1))
-    right[...] = right_matrix([parts[0]] * 7, power(c2, 7) * power(c3, 4))
+    right[...] = right_matrix([parts[0]] * 7, power(c2, 3) / 16)
     later_tables(parts, angle_parts(turn_ref, 1), angle_ref, later_left, later_right, later_rows)
+    for i in range(1, steps):
+        wave_copy(i).start()
     angle = angle_ref[0:1]
     elsewhere = device_bits()
+    level_copy.wait()
+
+    @pl.loop(0, BLOCKS // 2)
+    def _(i):
+        for j in range(2):
+            b = i * 2 + j
+            k = (elsewhere + count_bits(b, 4)) & 3
+            level = levels[pl.ds(b * 8, 8)]
+            out_ref[pl.ds(b * 8, 8), pl.ds(2 * CHUNK, CHUNK)] = level
+            co, si = cos_sin(level.reshape(ROWS, LANES) * angle)
+            swap = odd[k] > 0.5
+            cosines[b] = jnp.where(swap, si, co) * re_sign[k]
+            sines[b] = jnp.where(swap, co, si) * im_sign[k]
 
     @pl.loop(0, steps)
     def _(i):
-        level_copy(i).wait()
         wave_copy(i).wait()
         for j in range(per):
             b = i * per + j
-            k = (elsewhere + count_bits(b, 4)) & 3
-            level = out_ref[pl.ds(b * 8, 8), pl.ds(2 * CHUNK, CHUNK)].reshape(ROWS, LANES)
-            co, si = cos_sin(level * angle)
-            re, im = wave[i, 0, j], wave[i, 1, j]
-            swap = odd[k] > 0.5
-            u = jnp.where(swap, im, re) * re_sign[k]
-            v = jnp.where(swap, re, im) * im_sign[k]
-            re, im = mix_rows_lanes(u * co + v * si, v * co - u * si, left[...], right[...])
+            re, im, co, si = wave[i, 0, j], wave[i, 1, j], cosines[b], sines[b]
+            re, im = mix_rows_lanes(re * co + im * si, im * co - re * si, left[...], right[...])
             out_ref[pl.ds(b * 8, 8), pl.ds(0, CHUNK)] = re.reshape(8, CHUNK, LANES)
             out_ref[pl.ds(b * 8, 8), pl.ds(CHUNK, CHUNK)] = im.reshape(8, CHUNK, LANES)
 
-    t2 = jnp.broadcast_to(s2 / c2, (8, LANES))
-
-    mix_major(out_ref, out_ref, lambda k, at: k * 8 + at, [t2] * 4)
+    angles = [jnp.broadcast_to(row, (8, LANES)) for row in double_angles(c2, s2)]
+    mix_major(out_ref, out_ref, lambda k, at: k * 8 + at, angles)
 
 
 def middle_kernel(rows, left, right, in_ref, out_ref, held):
-    angle, t2 = rows[5, 0:1], rows[0, 0:1]
-    mix_major(in_ref, held, lambda k, at: at * 16 + k, [rows[1]] * 4)
+    angle, t2 = rows[0, 0:1], rows[1, 0:1]
+    mix_major(in_ref, held, lambda k, at: at * 16 + k, [rows[k] for k in range(3, 7)])
 
     @pl.loop(0, 16 // LOWS)
     def _(i):
@@ -219,27 +254,29 @@
             at = [h * 16 + low for h in range(8)]
             re = butterflies([held[k, pl.ds(0, CHUNK)] for k in at], [t2] * 3)
             im = butterflies([held[k, pl.ds(CHUNK, CHUNK)] for k in at], [t2] * 3)
-            turned = []
+            phased = []
             for h in range(8):
                 co, si = cos_sin(in_ref[at[h], pl.ds(2 * CHUNK, CHUNK)] * angle)
-                turned.append((re[h] * co + im[h] * si, im[h] * co - re[h] * si))
-            re, im = (jnp.concatenate(part, 0) for part in zip(*turned))
+                phased.append((re[h] * co + im[h] * si, im[h] * co - re[h] * si))
+            re, im = (jnp.concatenate(part, 0) for part in zip(*phased))
             re, im = mix_rows_lanes(re, im, left[...], right[...])
             for h in range(8):
                 held[at[h], pl.ds(0, CHUNK)] = re[h * CHUNK : (h + 1) * CHUNK]
                 held[at[h], pl.ds(CHUNK, CHUNK)] = im[h * CHUNK : (h + 1) * CHUNK]
 
-    mix_major(held, out_ref, lambda k, at: at * 16 + k, [rows[4]] * 4)
+    mix_major(held, out_ref, lambda k, at: at * 16 + k, [rows[k] for k in range(7, 11)])
 
 
 def last_kernel(rows, in_ref, out_ref, held, done, odd, re_sign, im_sign, sem):
-    t1, t2 = rows[2], rows[3]
+    t1, angles = rows[2], [rows[k] for k in range(11, 15)]
     set_phases(odd, re_sign, im_sign, CHUNK, 4, True)
     elsewhere = device_bits()
 
     def out_copy(half, b):
         return pltpu.make_async_copy(
-            done.at[:, b, :, half], out_ref.at[:, b, :, half], sem.at[half, b]
+            done.at[:, pl.ds(b * 4, 4), :, half],
+            out_ref.at[:, pl.ds(b * 4, 4), :, half],
+            sem.at[half, b],
         )
 
     for half in range(2):
@@ -251,13 +288,13 @@
                 for tile in (re_rows, im_rows):
                     at = i * 2 + j
                     values = [in_ref[b * 8 + at, tile] for b in range(BLOCKS)]
-                    for b, value in enumerate(butterflies(values, [t2] * 4)):
+                    for b, value in enumerate(mix_four(values, angles)):
                         held[b * 8 + at, tile] = value
 
-        @pl.loop(0, BLOCKS // 2)
+        @pl.loop(0, BLOCKS // 4)
         def _(i):
-            for j in range(2):
-                b = i * 2 + j
+            for j in range(4):
+                b = i * 4 + j
                 base = elsewhere + count_bits(b, 4)
                 re = butterflies([held[b * 8 + r, re_rows] for r in range(8)], [t1] * 3)
                 im = butterflies([held[b * 8 + r, im_rows] for r in range(8)], [t1] * 3)
@@ -266,13 +303,11 @@
                     swap = odd[k, re_rows] > 0.5
                     done[0, b, r, half] = jnp.where(swap, im[r], re[r]) * re_sign[k, re_rows]
                     done[1, b, r, half] = jnp.where(swap, re[r], im[r]) * im_sign[k, re_rows]
-            for j in range(2):
-                out_copy(half, i * 2 + j).start()
+            out_copy(half, i).start()
 
     for half in range(2):
 
-        @pl.loop(0, BLOCKS)
-        def _(b):
+        for b in range(BLOCKS // 4):
             out_copy(half, b).wait()
 
 
@@ -294,7 +329,7 @@
             jax.ShapeDtypeStruct((DEVICES, 3 * CHUNK, LANES), F32),
             jax.ShapeDtypeStruct(square, BF16),
             jax.ShapeDtypeStruct(square, BF16),
-            jax.ShapeDtypeStruct((6, 8, LANES), F32),
+            jax.ShapeDtypeStruct((15, 8, LANES), F32),
         ],
         in_specs=[hbm] * 4,
         out_specs=[vmem] * 4,
@@ -304,9 +339,10 @@
             pltpu.VMEM((STEPS, 2, BLOCKS // STEPS, ROWS, LANES), F32),
             pltpu.VMEM(square, BF16),
             pltpu.VMEM(square, BF16),
+            pltpu.VMEM((DEVICES, CHUNK, LANES), F32),
+            *[pltpu.VMEM((BLOCKS, ROWS, LANES), F32)] * 2,
             *[pltpu.VMEM((4, ROWS, LANES), F32)] * 3,
-            pltpu.SemaphoreType.DMA((2,)),
-            pltpu.SemaphoreType.DMA((STEPS,)),
+            pltpu.SemaphoreType.DMA((3,)),
             pltpu.SemaphoreType.DMA((STEPS,)),
         ],
     )(
@@ -343,7 +379,7 @@
             pltpu.VMEM((DEVICES, 2 * CHUNK, LANES), F32),
             pltpu.VMEM(tiled, F32),
             *[pltpu.VMEM((4, CHUNK, LANES), F32)] * 3,
-            pltpu.SemaphoreType.DMA((2, BLOCKS)),
+            pltpu.SemaphoreType.DMA((2, BLOCKS // 4)),
         ],
     )(rows, held)
     return out.reshape(2, BLOCKS, ROWS, LANES)

time: 96.8 us -> 96.1 us (level)
  no operation moved by 1% of the time
where the time goes in v3:
time: 96.1 us; the launch traced here: 95.9 us
  blocking collectives  86.1 us (90%)
  Pallas kernels  9.81 us (10%)
    all_to_all x2, blocking collectives, on_device(): held = lax.all_to_all(sent, HIGH_LOW, 0, 0, tiled=True)  86.1 us
    pallas_call x1, Pallas kernels, on_device(): pl.pallas_call(first_kernel, name='first', compiler_params=LIMIT, out_sha...  4.3 us
    pallas_call x1, Pallas kernels, on_device(): pl.pallas_call(middle_kernel, name='middle', compiler_params=LIMIT, out_s...  3.47 us
    pallas_call x1, Pallas kernels, on_device(): pl.pallas_call(last_kernel, name='last', compiler_params=LIMIT, out_shape...  2.05 us

profile of v3, /device:TPU:0, one launch (start us, length us, event | category | flops | bytes accessed | tf_op | source)
XLA Modules:
  0.0 95.9 jit_solution(14503805267695382230)
XLA Ops:
  0.0 4.3 %first.1 = (f32[128,48,128]{2,1,0:T(8,128)S(1)}, bf16[256,256]{1,0:T(8,128)(2,1)S(1)}, bf16[256,256]{1,0:T(8,128)(2,1)S(1)}, f32[15,8,128]{2,1,0:T(8,128)S(1)}) custom-call(f32[2,4]{1,0:T(2,128)} %turn_hbm.1, f32[2,128]{1,0:T(2,128)} %angle_hbm.1, f32[2,16,128,128]{3,2,1,0:T(8,128)} %wave_ref.1, f32[128,16,128]{2,1,0:T(8,128)} %bitcast.2), custom_call_target="tpu_custom_call" | custom-call | tf_op jit(solution)/shard_map/first/pallas_call | solution.py:324
  4.3 51.4 %all_to_all.10.in_ref = f32[128,48,128]{2,1,0:T(8,128)S(1)} all-to-all(f32[128,48,128]{2,1,0:T(8,128)S(1)} %get-tuple-element.12), channel_id=1, replica_groups=mesh['high'=8,'low'=16] {'high','low'}, dimensions={0} | all-to-all | bytes 6291456 | tf_op jit(solution)/shard_map/all_to_all | solution.py:359
  55.7 3.5 %middle.1 = f32[128,32,128]{2,1,0:T(8,128)S(1)} custom-call(f32[15,8,128]{2,1,0:T(8,128)S(1)} %get-tuple-element.9.rows, bf16[256,256]{1,0:T(8,128)(2,1)S(1)} %get-tuple-element.10.left, bf16[256,256]{1,0:T(8,128)(2,1)S(1)} %get-tuple-element.11.right, f32[128,48,128]{2,1,0:T(8,128)S(1)} %all_to_all.10.in_ref), custom_call_target="tpu_custom_call" | custom-call | tf_op jit(solution)/shard_map/middle/pallas_call | solution.py:360
  59.2 34.7 %all_to_all.11.in_ref = f32[128,32,128]{2,1,0:T(8,128)S(1)} all-to-all(f32[128,32,128]{2,1,0:T(8,128)S(1)} %middle.1), channel_id=1, replica_groups=mesh['high'=8,'low'=16] {'high','low'}, dimensions={0} | all-to-all | bytes 4194304 | tf_op jit(solution)/shard_map/all_to_all | solution.py:369
  93.9 2.0 %last.1 = f32[2,16,8,2,8,128]{5,4,3,2,1,0:T(8,128)} custom-call(f32[15,8,128]{2,1,0:T(8,128)S(1)} %get-tuple-element.9.rows, f32[128,32,128]{2,1,0:T(8,128)S(1)} %all_to_all.11.in_ref), custom_call_target="tpu_custom_call" | custom-call | tf_op jit(solution)/shard_map/last/pallas_call | solution.py:371

commit v4 on v3

--- a/solution.py
+++ b/solution.py
@@ -35,7 +35,7 @@
 
 
 def angle_parts(turn_ref, layer):
-    return [cos_sin(jnp.full((1, LANES), turn_ref[layer, g], F32)) for g in range(4)]
+    return [cos_sin(jnp.broadcast_to(turn_ref[layer : layer + 1, g : g + 1], (1, LANES))) for g in range(4)]
 
 
 def power(x, n):
@@ -334,7 +334,7 @@
         in_specs=[hbm] * 4,
         out_specs=[vmem] * 4,
         scratch_shapes=[
-            pltpu.SMEM((2, 4), F32),
+            pltpu.VMEM((2, 4), F32),
             pltpu.VMEM((2, LANES), F32),
             pltpu.VMEM((STEPS, 2, BLOCKS // STEPS, ROWS, LANES), F32),
             pltpu.VMEM(square, BF16),

time: 96.1 us -> 96.1 us (level)
  no operation moved by 1% of the time
where the time goes in v4:
time: 96.1 us; the launch traced here: 96 us
  blocking collectives  86.1 us (90%)
  Pallas kernels  9.83 us (10%)
    all_to_all x2, blocking collectives, on_device(): held = lax.all_to_all(sent, HIGH_LOW, 0, 0, tiled=True)  86.1 us
    pallas_call x1, Pallas kernels, on_device(): pl.pallas_call(first_kernel, name='first', compiler_params=LIMIT, out_sha...  4.32 us
    pallas_call x1, Pallas kernels, on_device(): pl.pallas_call(middle_kernel, name='middle', compiler_params=LIMIT, out_s...  3.47 us
    pallas_call x1, Pallas kernels, on_device(): pl.pallas_call(last_kernel, name='last', compiler_params=LIMIT, out_shape...  2.05 us

profile of v4, /device:TPU:0, one launch (start us, length us, event | category | flops | bytes accessed | tf_op | source)
XLA Modules:
  0.0 96.0 jit_solution(13313258117550771659)
XLA Ops:
  0.0 4.3 %first.1 = (f32[128,48,128]{2,1,0:T(8,128)S(1)}, bf16[256,256]{1,0:T(8,128)(2,1)S(1)}, bf16[256,256]{1,0:T(8,128)(2,1)S(1)}, f32[15,8,128]{2,1,0:T(8,128)S(1)}) custom-call(f32[2,4]{1,0:T(2,128)} %turn_hbm.1, f32[2,128]{1,0:T(2,128)} %angle_hbm.1, f32[2,16,128,128]{3,2,1,0:T(8,128)} %wave_ref.1, f32[128,16,128]{2,1,0:T(8,128)} %bitcast.2), custom_call_target="tpu_custom_call" | custom-call | tf_op jit(solution)/shard_map/first/pallas_call | solution.py:324
  4.3 51.4 %all_to_all.10.in_ref = f32[128,48,128]{2,1,0:T(8,128)S(1)} all-to-all(f32[128,48,128]{2,1,0:T(8,128)S(1)} %get-tuple-element.12), channel_id=1, replica_groups=mesh['high'=8,'low'=16] {'high','low'}, dimensions={0} | all-to-all | bytes 6291456 | tf_op jit(solution)/shard_map/all_to_all | solution.py:359
  55.7 3.5 %middle.1 = f32[128,32,128]{2,1,0:T(8,128)S(1)} custom-call(f32[15,8,128]{2,1,0:T(8,128)S(1)} %get-tuple-element.9.rows, bf16[256,256]{1,0:T(8,128)(2,1)S(1)} %get-tuple-element.10.left, bf16[256,256]{1,0:T(8,128)(2,1)S(1)} %get-tuple-element.11.right, f32[128,48,128]{2,1,0:T(8,128)S(1)} %all_to_all.10.in_ref), custom_call_target="tpu_custom_call" | custom-call | tf_op jit(solution)/shard_map/middle/pallas_call | solution.py:360
  59.2 34.7 %all_to_all.11.in_ref = f32[128,32,128]{2,1,0:T(8,128)S(1)} all-to-all(f32[128,32,128]{2,1,0:T(8,128)S(1)} %middle.1), channel_id=1, replica_groups=mesh['high'=8,'low'=16] {'high','low'}, dimensions={0} | all-to-all | bytes 4194304 | tf_op jit(solution)/shard_map/all_to_all | solution.py:369
  93.9 2.0 %last.1 = f32[2,16,8,2,8,128]{5,4,3,2,1,0:T(8,128)} custom-call(f32[15,8,128]{2,1,0:T(8,128)S(1)} %get-tuple-element.9.rows, f32[128,32,128]{2,1,0:T(8,128)S(1)} %all_to_all.11.in_ref), custom_call_target="tpu_custom_call" | custom-call | tf_op jit(solution)/shard_map/last/pallas_call | solution.py:371

commit v5 on v3

--- a/solution.py
+++ b/solution.py
@@ -194,14 +194,16 @@
             wave_ref.at[:, pl.ds(i * per, per)], wave.at[i], wave_sem.at[i]
         )
 
-    level_copy = pltpu.make_async_copy(
-        level_ref, levels, small_sem.at[2]
-    )
+    def level_copy(i):
+        part = pl.ds(i * 64, 64)
+        return pltpu.make_async_copy(level_ref.at[part], levels.at[part], small_sem.at[2 + i])
+
     turn_copy = pltpu.make_async_copy(turn_hbm, turn_ref, small_sem.at[0])
     angle_copy = pltpu.make_async_copy(angle_hbm, angle_ref, small_sem.at[1])
     turn_copy.start()
     angle_copy.start()
-    level_copy.start()
+    level_copy(0).start()
+    level_copy(1).start()
     set_phases(odd, re_sign, im_sign, ROWS, 7, True)
     wave_copy(0).start()
     turn_copy.wait()
@@ -210,28 +212,29 @@
     (c0, s0), (c1, s1), (c2, s2), (c3, s3) = parts
     left[...] = left_matrix([parts[1]] * 7, jnp.ones_like(c1))
     right[...] = right_matrix([parts[0]] * 7, power(c2, 3) / 16)
-    later_tables(parts, angle_parts(turn_ref, 1), angle_ref, later_left, later_right, later_rows)
     for i in range(1, steps):
         wave_copy(i).start()
     angle = angle_ref[0:1]
     elsewhere = device_bits()
-    level_copy.wait()
-
-    @pl.loop(0, BLOCKS // 2)
-    def _(i):
-        for j in range(2):
-            b = i * 2 + j
-            k = (elsewhere + count_bits(b, 4)) & 3
-            level = levels[pl.ds(b * 8, 8)]
-            out_ref[pl.ds(b * 8, 8), pl.ds(2 * CHUNK, CHUNK)] = level
-            co, si = cos_sin(level.reshape(ROWS, LANES) * angle)
-            swap = odd[k] > 0.5
-            cosines[b] = jnp.where(swap, si, co) * re_sign[k]
-            sines[b] = jnp.where(swap, co, si) * im_sign[k]
+    for half in range(2):
+        level_copy(half).wait()
+
+        @pl.loop(0, BLOCKS // 4)
+        def _(i):
+            for j in range(2):
+                b = half * 8 + i * 2 + j
+                k = (elsewhere + count_bits(b, 4)) & 3
+                level = levels[pl.ds(b * 8, 8)]
+                out_ref[pl.ds(b * 8, 8), pl.ds(2 * CHUNK, CHUNK)] = level
+                co, si = cos_sin(level.reshape(ROWS, LANES) * angle)
+                swap = odd[k] > 0.5
+                cosines[b] = jnp.where(swap, si, co) * re_sign[k]
+                sines[b] = jnp.where(swap, co, si) * im_sign[k]
 
     @pl.loop(0, steps)
     def _(i):
         wave_copy(i).wait()
+        later_tables(parts, angle_parts(turn_ref, 1), angle_ref, later_left, later_right, later_rows)
         for j in range(per):
             b = i * per + j
             re, im, co, si = wave[i, 0, j], wave[i, 1, j], cosines[b], sines[b]
@@ -342,7 +345,7 @@
             pltpu.VMEM((DEVICES, CHUNK, LANES), F32),
             *[pltpu.VMEM((BLOCKS, ROWS, LANES), F32)] * 2,
             *[pltpu.VMEM((4, ROWS, LANES), F32)] * 3,
-            pltpu.SemaphoreType.DMA((3,)),
+            pltpu.SemaphoreType.DMA((4,)),
             pltpu.SemaphoreType.DMA((STEPS,)),
         ],
     )(

time: 96.1 us -> 96.1 us (level)
  no operation moved by 1% of the time
where the time goes in v5:
time: 96.1 us; the launch traced here: 95.9 us
  blocking collectives  86.1 us (90%)
  Pallas kernels  9.81 us (10%)
    all_to_all x2, blocking collectives, on_device(): held = lax.all_to_all(sent, HIGH_LOW, 0, 0, tiled=True)  86.1 us
    pallas_call x1, Pallas kernels, on_device(): pl.pallas_call(first_kernel, name='first', compiler_params=LIMIT, out_sha...  4.3 us
    pallas_call x1, Pallas kernels, on_device(): pl.pallas_call(middle_kernel, name='middle', compiler_params=LIMIT, out_s...  3.47 us
    pallas_call x1, Pallas kernels, on_device(): pl.pallas_call(last_kernel, name='last', compiler_params=LIMIT, out_shape...  2.05 us

profile of v5, /device:TPU:0, one launch (start us, length us, event | category | flops | bytes accessed | tf_op | source)
XLA Modules:
  0.0 95.9 jit_solution(10725083257922919215)
XLA Ops:
  0.0 4.3 %first.1 = (f32[128,48,128]{2,1,0:T(8,128)S(1)}, bf16[256,256]{1,0:T(8,128)(2,1)S(1)}, bf16[256,256]{1,0:T(8,128)(2,1)S(1)}, f32[15,8,128]{2,1,0:T(8,128)S(1)}) custom-call(f32[2,4]{1,0:T(2,128)} %turn_hbm.1, f32[2,128]{1,0:T(2,128)} %angle_hbm.1, f32[2,16,128,128]{3,2,1,0:T(8,128)} %wave_ref.1, f32[128,16,128]{2,1,0:T(8,128)} %bitcast.2), custom_call_target="tpu_custom_call" | custom-call | tf_op jit(solution)/shard_map/first/pallas_call | solution.py:327
  4.3 51.4 %all_to_all.10.in_ref = f32[128,48,128]{2,1,0:T(8,128)S(1)} all-to-all(f32[128,48,128]{2,1,0:T(8,128)S(1)} %get-tuple-element.12), channel_id=1, replica_groups=mesh['high'=8,'low'=16] {'high','low'}, dimensions={0} | all-to-all | bytes 6291456 | tf_op jit(solution)/shard_map/all_to_all | solution.py:362
  55.7 3.5 %middle.1 = f32[128,32,128]{2,1,0:T(8,128)S(1)} custom-call(f32[15,8,128]{2,1,0:T(8,128)S(1)} %get-tuple-element.9.rows, bf16[256,256]{1,0:T(8,128)(2,1)S(1)} %get-tuple-element.10.left, bf16[256,256]{1,0:T(8,128)(2,1)S(1)} %get-tuple-element.11.right, f32[128,48,128]{2,1,0:T(8,128)S(1)} %all_to_all.10.in_ref), custom_call_target="tpu_custom_call" | custom-call | tf_op jit(solution)/shard_map/middle/pallas_call | solution.py:363
  59.2 34.7 %all_to_all.11.in_ref = f32[128,32,128]{2,1,0:T(8,128)S(1)} all-to-all(f32[128,32,128]{2,1,0:T(8,128)S(1)} %middle.1), channel_id=1, replica_groups=mesh['high'=8,'low'=16] {'high','low'}, dimensions={0} | all-to-all | bytes 4194304 | tf_op jit(solution)/shard_map/all_to_all | solution.py:372
  93.9 2.0 %last.1 = f32[2,16,8,2,8,128]{5,4,3,2,1,0:T(8,128)} custom-call(f32[15,8,128]{2,1,0:T(8,128)S(1)} %get-tuple-element.9.rows, f32[128,32,128]{2,1,0:T(8,128)S(1)} %all_to_all.11.in_ref), custom_call_target="tpu_custom_call" | custom-call | tf_op jit(solution)/shard_map/last/pallas_call | solution.py:374
